TPU v7x, 32 devices: a whole 2x2x4 slice. The times are simulated.
32 devices in a mesh: node: 16 (over z, x, core), local: 2 (over y).
Axes of the slice: x: 2, y: 2, z: 4, core: 2. Of those that a mesh axis runs over, the one named last changes fastest.
Arguments:
- tokens: bfloat16 [2, 16, 7168], P('local', 'node'), may hold values from -6 to 6
- node_ids: int32 [2, 16, 4], P('local', 'node'), may hold values from 0 to 7, all different within a row; in each aligned block of 16 rows (0 to 15, 16 to 31, ..., all dimensions but the last counted through in order) at most 9 rows name the same one
- gates: bfloat16 [2, 16, 8], P('local', 'node'), may hold values from 0.19921875 to 2
- w_in: bfloat16 [32, 3584, 4096], P(('node', 'local')), may hold values from -0.0625 to 0.0625
- w_out: bfloat16 [16, 2048, 7168], P('node', 'local'), may hold values from -0.125 to 0.125
Outputs:
- mixed: bfloat16 [2, 16, 7168], P('local', 'node')
- balance: float32 [16], P('node')
Inputs may be any that keep to these rules, and one draw needn't show every extreme that they name: `node_ids`: each token names 4 different nodes. Among the 16 tokens of one index along the first dimension, no node is named by more than 9 tokens, and in every draw, for some index, some node is named by exactly 9 of them.
All inputs are finite; a program needn't handle non-finite values.
Results may differ from a plain program's by a relative error of at most 0.017.
Values may be sent and summed in bfloat16 or wider, within the bound.
A program may use at most 128 MiB of HBM per device.

v0:
```python
import functools

import jax
import jax.numpy as jnp
from jax import lax
from jax.experimental import pallas as pl
from jax.experimental.pallas import tpu as pltpu
from jax.sharding import PartitionSpec as P

NODE_TOP = 4


def swapped(value, axis, apart):
    mask = 2**apart
    pairs = [(source, source ^ mask) for source in range(lax.axis_size(axis))]
    return lax.ppermute(value, axis, pairs)


def packing(flat_gate, capacity):
    live = flat_gate > 0
    order = jnp.cumsum(live.astype(jnp.int32)) - 1
    wanted = jnp.arange(capacity, dtype=jnp.int32)[:, None]
    return (live[None, :] & (order[None, :] == wanted)).astype(jnp.bfloat16)


def shards(tokens, node_ids, gates, w_in, w_out):
    nodes = lax.axis_size("node")
    local_count = lax.axis_size("local")
    parity = lax.axis_index("local") % 2
    own = tokens[0]
    routes = node_ids[0]
    tok_count = own.shape[0]
    model = own.shape[1]
    half = model // 2
    groups = nodes // 2
    capacity = tok_count * min(nodes, 2 * NODE_TOP + 1)
    slots = nodes * tok_count
    pair_gates = gates[0].astype(jnp.float32).reshape(tok_count, NODE_TOP, 2)
    member = routes[:, :, None] == jnp.arange(groups, dtype=jnp.int32)
    group_visits = jnp.any(member, axis=1)
    row_visits = jnp.repeat(group_visits, 2, axis=1)
    expert_gate = jnp.sum(
        jnp.where(member[:, :, :, None], pair_gates[:, :, None, :], jnp.float32(0.0)), axis=1
    ).reshape(tok_count, nodes)
    gate_out = expert_gate.T.astype(jnp.bfloat16)
    outbound = jnp.where(row_visits.T[:, :, None], own[None], jnp.zeros((), own.dtype))
    arrived, arrived_gate = (
        lax.all_to_all(outbound, "node", split_axis=0, concat_axis=0, tiled=True),
        lax.all_to_all(gate_out, "node", split_axis=0, concat_axis=0, tiled=True),
    )
    flat_gate = arrived_gate.reshape(slots)
    select = packing(flat_gate, capacity)
    packed = jnp.dot(
        select, arrived.reshape(slots, model), preferred_element_type=jnp.float32
    ).astype(jnp.bfloat16)
    packed_gate = jnp.dot(select, flat_gate[:, None], preferred_element_type=jnp.float32)[
        :, 0
    ].astype(jnp.bfloat16)
    outgoing = jnp.tile(
        packed.reshape(capacity, 2, half).transpose(1, 0, 2), (local_count // 2, 1, 1)
    )
    gate_copies = jnp.broadcast_to(packed_gate[None, :], (local_count, capacity))
    parts, gate_parts = (
        lax.all_to_all(outgoing, "local", split_axis=0, concat_axis=0, tiled=True),
        lax.all_to_all(gate_copies, "local", split_axis=0, concat_axis=0, tiled=True),
    )
    my_rows = parts.reshape(local_count * capacity, half)
    row_gate = gate_parts.reshape(local_count * capacity)
    partial_value = jnp.dot(my_rows, w_in[0], preferred_element_type=jnp.float32)
    summed_pre = partial_value + swapped(partial_value, "local", 0)
    ff_dev = w_in.shape[2] // 2
    hidden = (
        row_gate.astype(jnp.float32)[:, None]
        * jax.nn.silu(summed_pre[:, :ff_dev])
        * summed_pre[:, ff_dev:]
    ).astype(jnp.bfloat16)
    block = w_out.shape[1]
    mine = lax.dynamic_slice_in_dim(hidden, parity * block, block, 1)
    expert_rows = lax.psum_scatter(
        jnp.dot(mine, w_out[0], preferred_element_type=jnp.float32).astype(jnp.bfloat16),
        "local",
        scatter_dimension=0,
        tiled=True,
    )
    unpacked = jnp.dot(select.T, expert_rows, preferred_element_type=jnp.float32).astype(
        jnp.bfloat16
    )
    returned = lax.all_to_all(
        unpacked.reshape(nodes, tok_count, model), "node", split_axis=0, concat_axis=0, tiled=True
    )
    mixed = jnp.sum(returned.astype(jnp.float32), axis=0).astype(jnp.bfloat16)[None]
    tokens_all = tok_count * nodes * local_count
    scale = jnp.float32(nodes / (2 * NODE_TOP * tokens_all))
    counted, gate_total = lax.psum(
        (jnp.sum(row_visits.astype(jnp.float32), axis=0), jnp.sum(expert_gate, axis=0)),
        ("node", "local"),
    )
    counted = lax.dynamic_slice_in_dim(counted, lax.axis_index("node"), 1, 0)
    gate_total = lax.dynamic_slice_in_dim(gate_total, lax.axis_index("node"), 1, 0)
    balance = counted * scale * (gate_total * scale)
    return (mixed, balance)


LANES = 128
F32 = jnp.float32
BF16 = jnp.bfloat16
W_IN_PIECES = 1
W_OUT_PIECES = 1
MESH = pl.DeviceIdType.MESH


def body_of_pair(
    sizes,
    tok_ref, ids_ref, gate_ref, win_ref, wout_ref, mix_ref, bal_ref,
    w1, w2, tstage, msg, xbuf, xstage, xmat, ysend, yrecv, pre, hid, acc, asend, arecv, ostage, bsend,
    brecv, fstage,
    w1_sem, w2_sem, d_send, d_recv, f_send, f_recv, y_send, y_recv, a_send, a_recv, b_send, b_recv,
):
    nodes, half, ff, block, model = sizes
    node, mine = lax.axis_index("node"), lax.axis_index("local")
    core, chip = lax.rem(node, 2), lax.div(node, 2)
    peers = nodes
    me = chip * 2 + mine
    rows, wide = 2 * peers, xbuf.shape[1]
    sub = half // LANES
    piece = block // W_IN_PIECES
    cols = model // W_OUT_PIECES
    osub = cols // LANES
    opad = bsend.shape[2]
    mate = {"node": 2 * chip + 1 - core, "local": mine}
    twin = {"node": node, "local": 1 - mine}

    def peer(p):
        return {"node": 2 * lax.div(p, 2) + core, "local": lax.rem(p, 2)}

    def w1_copy(i):
        far, j, part = i // (2 * W_IN_PIECES), (i // 2) % W_IN_PIECES, i % 2
        owner = mine if far else 1 - mine
        off = pl.multiple_of(part * ff + owner * block + j * piece, piece)
        return pltpu.make_async_copy(win_ref.at[0, :, pl.ds(off, piece)], w1.at[i], w1_sem.at[i])

    def w2_copy(j):
        return pltpu.make_async_copy(
            wout_ref.at[0, :, pl.ds(j * cols, cols)], w2.at[j], w2_sem.at[j]
        )

    for i in range(4 * W_IN_PIECES):
        w1_copy(i).start()
    for j in range(W_OUT_PIECES):
        w2_copy(j).start()

    barrier = pltpu.get_barrier_semaphore()

    def greet(k, _):
        pl.semaphore_signal(
            barrier, inc=1, device_id=peer(lax.rem(me + k, peers)), device_id_type=MESH
        )
        return 0

    lax.fori_loop(1, peers, greet, 0)
    pl.semaphore_signal(barrier, inc=1, device_id=mate, device_id_type=MESH)

    lane = lax.broadcasted_iota(jnp.int32, (1, LANES), 1)
    ids, gates = ids_ref[0], gate_ref[0].astype(F32)
    weight = jnp.zeros((1, LANES), F32)
    for m in range(NODE_TOP):
        pair = jnp.where(lane % 2 == 0, gates[:, 2 * m : 2 * m + 1], gates[:, 2 * m + 1 : 2 * m + 2])
        weight += jnp.where(lane // 2 == ids[:, m : m + 1], pair, 0.0)
    tstage[...] = jnp.zeros_like(tstage)
    for h in range(2):
        for k in range(sub):
            at = h * half + k * LANES
            tstage[h * wide + k : h * wide + k + 1, :] = tok_ref[0, :, at : at + LANES].astype(F32)
        tstage[h * wide + sub : h * wide + sub + 1, :] = weight
        msg[h] = tstage[h * wide : (h + 1) * wide, :].astype(BF16)
    xbuf[me] = msg[mine]
    ostage[...] = jnp.zeros_like(ostage)

    pl.semaphore_wait(barrier, peers)

    def d_copy(k, p, slot):
        return pltpu.make_async_remote_copy(
            src_ref=msg.at[lax.rem(p, 2)], dst_ref=xbuf.at[slot], send_sem=d_send.at[k],
            recv_sem=d_recv.at[slot], device_id=peer(p), device_id_type=MESH,
        )

    def f_copy(p):
        return pltpu.make_async_remote_copy(
            src_ref=xbuf.at[p], dst_ref=xbuf.at[peers + p], send_sem=f_send.at[p],
            recv_sem=f_recv.at[p], device_id=mate, device_id_type=MESH,
        )

    def send_token(k, _):
        d_copy(k, lax.rem(me + k, peers), me).start()
        return 0

    lax.fori_loop(1, peers, send_token, 0)
    f_copy(me).start()

    def pass_on(k, _):
        p = lax.rem(me + peers - k, peers)
        d_copy(k, p, p).wait_recv()
        f_copy(p).start()
        return 0

    lax.fori_loop(1, peers, pass_on, 0)

    def widen(t, _):
        xstage[pl.ds(pl.multiple_of(t * wide, wide), wide), :] = xbuf[t].astype(F32)
        return 0

    lax.fori_loop(0, peers, widen, 0)

    def widen_far(t, _):
        f_copy(t).wait_recv()
        return widen(t + peers, 0)

    lax.fori_loop(0, peers, widen_far, 0)
    for k in range(sub):
        xmat[:, k * LANES : (k + 1) * LANES] = xstage[pl.ds(k, rows, stride=wide), :].astype(BF16)
    all_gates = xstage[pl.ds(sub, rows, stride=wide), :]
    lanes = lax.broadcasted_iota(jnp.int32, (rows, LANES), 1)
    own_gate = jnp.sum(jnp.where(lanes == node, all_gates, 0.0), axis=1, keepdims=True)

    def y_copy(i):
        return pltpu.make_async_remote_copy(
            src_ref=ysend.at[i], dst_ref=yrecv.at[i], send_sem=y_send.at[i],
            recv_sem=y_recv.at[i], device_id=twin, device_id_type=MESH,
        )

    def w1_wait(i):
        pltpu.make_async_copy(w1.at[i], w1.at[i], w1_sem.at[i]).wait()

    def project_far(i, _):
        w1_wait(i)
        ysend[i] = jnp.dot(xmat[...], w1[i], preferred_element_type=F32).astype(BF16)
        y_copy(i).start()
        return 0

    lax.fori_loop(0, 2 * W_IN_PIECES, project_far, 0)

    def project_own(i, _):
        w1_wait(2 * W_IN_PIECES + i)
        pre[i] = jnp.dot(xmat[...], w1[2 * W_IN_PIECES + i], preferred_element_type=F32)
        return 0

    lax.fori_loop(0, 2 * W_IN_PIECES, project_own, 0)

    def activate(j, _):
        y_copy(2 * j).wait_recv()
        y_copy(2 * j + 1).wait_recv()
        gate_part = pre[2 * j] + yrecv[2 * j].astype(F32)
        up_part = pre[2 * j + 1] + yrecv[2 * j + 1].astype(F32)
        value = own_gate * (gate_part / (1.0 + jnp.exp(-gate_part))) * up_part
        hid[:, pl.ds(pl.multiple_of(j * piece, piece), piece)] = value.astype(BF16)
        return 0

    lax.fori_loop(0, W_IN_PIECES, activate, 0)

    def a_copy(j):
        return pltpu.make_async_remote_copy(
            src_ref=asend.at[j], dst_ref=arecv.at[j], send_sem=a_send.at[j],
            recv_sem=a_recv.at[j], device_id=mate, device_id_type=MESH,
        )

    def b_copy(j, p, slot):
        return pltpu.make_async_remote_copy(
            src_ref=bsend.at[j, p], dst_ref=brecv.at[j, slot], send_sem=b_send.at[j, p],
            recv_sem=b_recv.at[j, slot], device_id=peer(p), device_id_type=MESH,
        )

    def finish(j):
        a_copy(j).wait_recv()
        total = acc[j] + arecv[j].astype(F32)
        for q in range(osub):
            ostage[pl.ds(q, peers, stride=opad), :] = total[:, q * LANES : (q + 1) * LANES]
        for p in range(peers):
            bsend[j, p] = ostage[p * opad : (p + 1) * opad, :].astype(BF16)

        def send_row(k, _):
            b_copy(j, lax.rem(me + k, peers), me).start()
            return 0

        lax.fori_loop(1, peers, send_row, 0)
        brecv[j, me] = bsend[j, me]

    def down(j, _):
        pltpu.make_async_copy(w2.at[j], w2.at[j], w2_sem.at[j]).wait()
        part = jnp.dot(hid[...], w2[j], preferred_element_type=F32)
        asend[j] = part[peers:].astype(BF16)
        acc[j] = part[:peers]
        a_copy(j).start()

        @pl.when(j > 0)
        def _():
            finish(j - 1)

        return 0

    lax.fori_loop(0, W_OUT_PIECES, down, 0)
    finish(W_OUT_PIECES - 1)

    tokens_all = 2.0 * nodes
    scale = nodes / (2 * NODE_TOP * tokens_all)
    count = jnp.sum((own_gate > 0).astype(F32))
    bal_ref[0] = (count * scale) * (jnp.sum(own_gate) * scale)

    for j in range(W_OUT_PIECES):

        def arrive(k, _, j=j):
            p = lax.rem(me + peers - k, peers)
            b_copy(j, p, p).wait_recv()
            return 0

        lax.fori_loop(1, peers, arrive, 0)
        fstage[...] = jnp.sum(brecv[j].astype(F32), axis=0)
        line = jnp.concatenate([fstage[q : q + 1, :] for q in range(osub)], axis=1)
        mix_ref[0, :, j * cols : (j + 1) * cols] = line.astype(BF16)

    def settle(k, _):
        p = lax.rem(me + k, peers)
        d_copy(k, p, me).wait_send()
        for j in range(W_OUT_PIECES):
            b_copy(j, p, me).wait_send()
        return 0

    lax.fori_loop(1, peers, settle, 0)

    def settle_mate(p, _):
        f_copy(p).wait_send()
        return 0

    lax.fori_loop(0, peers, settle_mate, 0)
    for i in range(2 * W_IN_PIECES):
        y_copy(i).wait_send()
    for j in range(W_OUT_PIECES):
        a_copy(j).wait_send()


def fused(tokens, node_ids, gates, w_in, w_out):
    nodes = lax.axis_size("node")
    model, half, ff, block = tokens.shape[2], w_in.shape[1], w_in.shape[2] // 2, w_out.shape[1]
    rows, peers = 2 * nodes, nodes
    sub = half // LANES
    wide = -(-(sub + 1) // 16) * 16
    piece, cols = block // W_IN_PIECES, model // W_OUT_PIECES
    opad = -(-(cols // LANES) // 8) * 8
    sem = pltpu.SemaphoreType.DMA
    vmem = pl.BlockSpec(memory_space=pltpu.VMEM)
    anywhere = pl.BlockSpec(memory_space=pl.ANY)
    return tuple(pl.pallas_call(
        functools.partial(body_of_pair, (nodes, half, ff, block, model)),
        out_shape=(
            jax.ShapeDtypeStruct(tokens.shape, BF16),
            jax.ShapeDtypeStruct((1,), F32),
        ),
        in_specs=[vmem, vmem, vmem, anywhere, anywhere],
        out_specs=(vmem, pl.BlockSpec(memory_space=pltpu.SMEM)),
        scratch_shapes=[
            pltpu.VMEM((4 * W_IN_PIECES, half, piece), BF16),
            pltpu.VMEM((W_OUT_PIECES, block, cols), BF16),
            pltpu.VMEM((2 * wide, LANES), F32),
            pltpu.VMEM((2, wide, LANES), BF16),
            pltpu.VMEM((rows, wide, LANES), BF16),
            pltpu.VMEM((rows * wide, LANES), F32),
            pltpu.VMEM((rows, half), BF16),
            pltpu.VMEM((2 * W_IN_PIECES, rows, piece), BF16),
            pltpu.VMEM((2 * W_IN_PIECES, rows, piece), BF16),
            pltpu.VMEM((2 * W_IN_PIECES, rows, piece), F32),
            pltpu.VMEM((rows, block), BF16),
            pltpu.VMEM((W_OUT_PIECES, peers, cols), F32),
            pltpu.VMEM((W_OUT_PIECES, peers, cols), BF16),
            pltpu.VMEM((W_OUT_PIECES, peers, cols), BF16),
            pltpu.VMEM((peers * opad, LANES), F32),
            pltpu.VMEM((W_OUT_PIECES, peers, opad, LANES), BF16),
            pltpu.VMEM((W_OUT_PIECES, peers, opad, LANES), BF16),
            pltpu.VMEM((opad, LANES), F32),
            sem((4 * W_IN_PIECES,)),
            sem((W_OUT_PIECES,)),
            sem((peers,)),
            sem((peers,)),
            sem((peers,)),
            sem((peers,)),
            sem((2 * W_IN_PIECES,)),
            sem((2 * W_IN_PIECES,)),
            sem((W_OUT_PIECES,)),
            sem((W_OUT_PIECES,)),
            sem((W_OUT_PIECES, peers)),
            sem((W_OUT_PIECES, peers)),
        ],
        compiler_params=pltpu.CompilerParams(
            collective_id=0, has_side_effects=True, vmem_limit_bytes=60 * 1024 * 1024
        ),
    )(tokens, node_ids, gates, w_in, w_out))


def solution(mesh):
    placed = (
        P("local", "node", None),
        P("local", "node", None),
        P("local", "node", None),
        P(("node", "local"), None, None),
        P("node", "local", None),
    )
    body = fused if mesh.shape["local"] == 2 and mesh.shape["node"] % 2 == 0 else shards
    return jax.shard_map(
        body,
        mesh=mesh,
        in_specs=placed,
        out_specs=(P("local", "node", None), P("node")),
        check_vma=False,
    )
```

profile of v0, /device:TPU:0, one launch (start us, length us, event | category | flops | bytes accessed | tf_op | source)
XLA Modules:
  0.0 34.7 jit_solution(6631551594724257594)
XLA Ops:
  0.6 30.9 %shard_map.68 = (bf16[1,1,7168]{2,1,0:T(2,128)(2,1)}, f32[1]{0:T(128)}) custom-call(bf16[1,1,7168]{2,1,0:T(2,128)(2,1)} %tok_ref.1, s32[1,1,4]{2,1,0:T(1,128)} %ids_ref.1, bf16[1,1,8]{2,1,0:T(2,128)(2,1)} %gate_ref.1, bf16[1,3584,4096]{2,1,0:T(8,128)(2,1)} %win_ref.1, bf16[1,1024,7168]{2,1,0:T(8,128)(2,1)} %wout_ref.1), custom_call_target="tpu_custom_call" | custom-call | tf_op jit(solution)/shard_map/pallas_call | solution.py:351
  31.6 1.4 %copy.9 = bf16[1,1,7168]{2,1,0:T(2,128)(2,1)} copy(bf16[1,1,7168]{2,1,0:T(2,128)(2,1)} %get-tuple-element.4) | data formatting | bytes 28672
where the time goes:
time: 35 us; the launch traced here: 34.7 us
  Pallas kernels  30.9 us (88%)
  between operations  2.4 us (7%)
  local copies, waits for them, and re-layouts  1.39 us (4%)
    pallas_call x1, Pallas kernels, fused(): pl.pallas_call(functools.partial(body_of_pair, (nodes, half, ff, block, m...  30.9 us
    unnamed x1, local copies, waits for them, and re-layouts  1.39 us

commit v1 on v0

--- a/solution.py
+++ b/solution.py
@@ -111,10 +111,10 @@
 
 def body_of_pair(
     sizes,
-    tok_ref, ids_ref, gate_ref, win_ref, wout_ref, mix_ref, bal_ref,
-    w1, w2, tstage, msg, xbuf, xstage, xmat, ysend, yrecv, pre, hid, acc, asend, arecv, ostage, bsend,
+    tok_hbm, ids_hbm, gate_hbm, win_ref, wout_ref, mix_ref, bal_ref,
+    tok_ref, ids_ref, gate_ref, w1, w2, tstage, msg, xbuf, xstage, xmat, ysend, yrecv, pre, hid, acc, asend, arecv, ostage, bsend,
     brecv, fstage,
-    w1_sem, w2_sem, d_send, d_recv, f_send, f_recv, y_send, y_recv, a_send, a_recv, b_send, b_recv,
+    in_sem, w1_sem, w2_sem, d_send, d_recv, f_send, f_recv, y_send, y_recv, a_send, a_recv, b_send, b_recv,
 ):
     nodes, half, ff, block, model = sizes
     node, mine = lax.axis_index("node"), lax.axis_index("local")
@@ -144,11 +144,6 @@
             wout_ref.at[0, :, pl.ds(j * cols, cols)], w2.at[j], w2_sem.at[j]
         )
 
-    for i in range(4 * W_IN_PIECES):
-        w1_copy(i).start()
-    for j in range(W_OUT_PIECES):
-        w2_copy(j).start()
-
     barrier = pltpu.get_barrier_semaphore()
 
     def greet(k, _):
@@ -159,6 +154,21 @@
 
     lax.fori_loop(1, peers, greet, 0)
     pl.semaphore_signal(barrier, inc=1, device_id=mate, device_id_type=MESH)
+
+    inputs = [
+        pltpu.make_async_copy(source, target, in_sem.at[i])
+        for i, (source, target) in enumerate(
+            ((ids_hbm, ids_ref), (gate_hbm, gate_ref), (tok_hbm, tok_ref))
+        )
+    ]
+    for copy in inputs:
+        copy.start()
+    for i in range(4 * W_IN_PIECES):
+        w1_copy(i).start(priority=1)
+    for j in range(W_OUT_PIECES):
+        w2_copy(j).start(priority=1)
+    for copy in inputs:
+        copy.wait()
 
     lane = lax.broadcasted_iota(jnp.int32, (1, LANES), 1)
     ids, gates = ids_ref[0], gate_ref[0].astype(F32)
@@ -347,16 +357,18 @@
     opad = -(-(cols // LANES) // 8) * 8
     sem = pltpu.SemaphoreType.DMA
     vmem = pl.BlockSpec(memory_space=pltpu.VMEM)
-    anywhere = pl.BlockSpec(memory_space=pl.ANY)
     return tuple(pl.pallas_call(
         functools.partial(body_of_pair, (nodes, half, ff, block, model)),
         out_shape=(
-            jax.ShapeDtypeStruct(tokens.shape, BF16),
-            jax.ShapeDtypeStruct((1,), F32),
+            pltpu.VMEM(tokens.shape, BF16),
+            pltpu.SMEM((1,), F32),
         ),
-        in_specs=[vmem, vmem, vmem, anywhere, anywhere],
+        in_specs=[pl.BlockSpec(memory_space=pltpu.HBM)] * 5,
         out_specs=(vmem, pl.BlockSpec(memory_space=pltpu.SMEM)),
         scratch_shapes=[
+            pltpu.VMEM(tokens.shape, BF16),
+            pltpu.VMEM(node_ids.shape, jnp.int32),
+            pltpu.VMEM(gates.shape, BF16),
             pltpu.VMEM((4 * W_IN_PIECES, half, piece), BF16),
             pltpu.VMEM((W_OUT_PIECES, block, cols), BF16),
             pltpu.VMEM((2 * wide, LANES), F32),
@@ -375,6 +387,7 @@
             pltpu.VMEM((W_OUT_PIECES, peers, opad, LANES), BF16),
             pltpu.VMEM((W_OUT_PIECES, peers, opad, LANES), BF16),
             pltpu.VMEM((opad, LANES), F32),
+            sem((3,)),
             sem((4 * W_IN_PIECES,)),
             sem((W_OUT_PIECES,)),
             sem((peers,)),

time: 35 us -> 31.6 us (0.903)
  between operations: 2.4 us -> 1.16 us
  Pallas kernels: 30.9 us -> 29.7 us
  local copies, waits for them, and re-layouts: 1.39 us -> 0.61 us
    pallas_call x1, Pallas kernels: 30.9 us -> 29.7 us  [fused(): pl.pallas_call(functools.partial(body_of_pair, (nodes, half, ff, block, m...]
    unnamed x1, local copies, waits for them, and re-layouts: 1.39 us -> 0.61 us
where the time goes in v1:
time: 31.6 us; the launch traced here: 31.5 us
  Pallas kernels  29.7 us (94%)
  between operations  1.16 us (4%)
  local copies, waits for them, and re-layouts  0.61 us (2%)
    pallas_call x1, Pallas kernels, fused(): pl.pallas_call(functools.partial(body_of_pair, (nodes, half, ff, block, m...  29.7 us

profile of v1, /device:TPU:0, one launch (start us, length us, event | category | flops | bytes accessed | tf_op | source)
XLA Modules:
  0.0 31.5 jit_solution(893402165210116009)
XLA Ops:
  0.6 29.7 %shard_map.68 = (bf16[1,1,7168]{2,1,0:T(2,128)(2,1)S(1)}, f32[1]{0:T(128)S(4)}) custom-call(bf16[1,1,7168]{2,1,0:T(2,128)(2,1)} %tok_hbm.1, s32[1,1,4]{2,1,0:T(1,128)} %ids_hbm.1, bf16[1,1,8]{2,1,0:T(2,128)(2,1)} %gate_hbm.1, bf16[1,3584,4096]{2,1,0:T(8,128)(2,1)} %win_ref.1, bf16[1,1024,7168]{2,1,0:T(8,128)(2,1)} %wout_ref.1), custom_call_target="tpu_custom_call" | custom-call | tf_op jit(solution)/shard_map/pallas_call | solution.py:360
  30.9 0.6 %copy.9 = bf16[1,1,7168]{2,1,0:T(2,128)(2,1)} copy(bf16[1,1,7168]{2,1,0:T(2,128)(2,1)S(1)} %get-tuple-element.2) | data formatting | bytes 28672
